TPU v7x, 32 devices: a whole 2x2x4 slice. The times are simulated.
32 devices in a mesh: seq: 8 (over z, y), mp: 4 (over x, core).
Axes of the slice: x: 2, y: 2, z: 4, core: 2. Of those that a mesh axis runs over, the one named last changes fastest.
Arguments:
- gate_in: bfloat16 [8192, 1024], P('seq', 'mp'), may hold values from -5 to 5
- value_in: bfloat16 [8192, 1024], P('seq', 'mp'), may hold values from -5 to 5
- out_gate: bfloat16 [8192, 1024], P('seq', 'mp'), may hold values from -10 to 10
- filter_taps: bfloat16 [4096, 1024], P('seq', 'mp'), may hold values from -0.09375 to 0.09375
- skip_gain: float32 [1024], P('mp'), may hold values from -4 to 4
Outputs:
- output: bfloat16 [8192, 1024], P('seq', 'mp')
All inputs are finite; a program needn't handle non-finite values.
Results may differ from a plain program's by a relative error of at most 0.009.
Values may be sent and summed in bfloat16 or wider, within the bound.
A program may use at most 64 MiB of HBM per device.

v0:
```python
import math

import jax
import jax.numpy as jnp
from jax import lax
from jax.sharding import PartitionSpec as P

C = 1024
K = 4096
P_SIZE = 128


def shortened(shard):
    return jax.tree.map(lambda a: a.astype(jnp.bfloat16) if a.dtype == jnp.float32 else a, shard)


def dft_tables(block):
    frame_len = 2 * block
    sample = lax.iota(jnp.int32, frame_len)[:, None]
    frequency = lax.iota(jnp.int32, block)[None, :]
    angles = (sample * frequency % frame_len).astype(jnp.float32) * (2.0 * math.pi / frame_len)
    alternate = jnp.where(sample % 2 == 0, 1.0, -1.0).astype(jnp.float32)
    forward = jnp.concatenate(
        [jnp.cos(angles), jnp.where(frequency == 0, alternate, -jnp.sin(angles))], axis=1
    )
    later = block + lax.iota(jnp.int32, block)[None, :]
    column = lax.iota(jnp.int32, block)[:, None]
    back_angles = (column * later % frame_len).astype(jnp.float32) * (2.0 * math.pi / frame_len)
    back_sign = jnp.where(later % 2 == 0, 1.0, -1.0).astype(jnp.float32)
    inv_real = jnp.where(column == 0, 1.0, 2.0 * jnp.cos(back_angles)) / frame_len
    inv_imag = jnp.where(column == 0, back_sign, -2.0 * jnp.sin(back_angles)) / frame_len
    backward = jnp.concatenate([inv_real, inv_imag], axis=0)
    return (forward, backward)


def split_table(table):
    upper_part = table.astype(jnp.bfloat16)
    lower_part = (table - upper_part.astype(jnp.float32)).astype(jnp.bfloat16)
    return (upper_part, lower_part)


def transform_rows(form, data, table):
    upper_part, lower_part = split_table(table)
    first = jnp.einsum(form, data, upper_part, preferred_element_type=jnp.float32)
    return first + jnp.einsum(form, data, lower_part, preferred_element_type=jnp.float32)


def filter_spectra(portion):
    forward, backward = dft_tables(P_SIZE)
    channels = portion.shape[1]
    segments = portion.reshape(-1, P_SIZE, channels)
    return transform_rows("snc,nf->scf", segments, forward[:P_SIZE])


def convolve(window, filter_spec):
    forward, backward = dft_tables(P_SIZE)
    channels = window.shape[1]
    blocks = window.reshape(-1, P_SIZE, channels)
    frames = jnp.concatenate([blocks[:-1], blocks[1:]], axis=1)
    spectra = transform_rows("mnc,nf->mcf", frames, forward)
    frame_count = spectra.shape[0]
    seg_count = filter_spec.shape[0]
    features = channels * 2 * P_SIZE
    lhs_data = spectra.reshape(1, frame_count, features)
    spec_real = filter_spec[..., :P_SIZE]
    spec_imag = filter_spec[..., P_SIZE:]
    kernel_real = jnp.concatenate([spec_real, spec_real], axis=-1)
    kernel_imag = jnp.concatenate([spec_imag, spec_imag], axis=-1)
    kernel = jnp.stack([kernel_real, kernel_imag], axis=-1)[::-1].reshape(
        seg_count, 1, features * 2
    )
    merged = lax.conv_general_dilated(
        lhs_data,
        kernel,
        (1,),
        "VALID",
        dimension_numbers=("NWC", "WIO", "NWC"),
        feature_group_count=features,
        precision=lax.Precision.HIGH,
    )
    merged = merged.reshape(-1, channels, 2 * P_SIZE, 2)
    with_real = merged[..., 0]
    with_imag = merged[..., 1]
    first_col = lax.iota(jnp.int32, P_SIZE) == 0
    out_real = with_real[..., :P_SIZE] - jnp.where(first_col, 0.0, with_imag[..., P_SIZE:])
    out_imag = jnp.where(
        first_col, with_imag[..., P_SIZE:], with_imag[..., :P_SIZE] + with_real[..., P_SIZE:]
    )
    joined = jnp.concatenate([out_real, out_imag], axis=-1)
    result = jnp.einsum("bcf,fn->bnc", joined, backward, precision=lax.Precision.HIGH)
    return result.reshape(-1, channels)


def local(gate_in, value_in, out_gate, filter_taps, skip_gain):
    gated = (gate_in.astype(jnp.float32) * value_in.astype(jnp.float32)).astype(jnp.bfloat16)
    by_channel, taps_channel = (
        lax.all_to_all(gated, "seq", split_axis=1, concat_axis=0, tiled=True),
        lax.all_to_all(filter_taps, "seq", split_axis=1, concat_axis=0, tiled=True),
    )
    leading = jnp.zeros((K, by_channel.shape[1]), jnp.bfloat16)
    window = jnp.concatenate([leading, by_channel], axis=0)
    filter_spec = filter_spectra(taps_channel)
    channel_result = convolve(window, filter_spec)
    convolved = lax.all_to_all(
        shortened(channel_result), "seq", split_axis=0, concat_axis=1, tiled=True
    ).astype(channel_result.dtype)
    gated_out = out_gate.astype(jnp.float32) * (
        convolved + skip_gain[None, :] * gated.astype(jnp.float32)
    )
    squares = jnp.sum(gated_out * gated_out, axis=1)
    totals = lax.psum(squares, "mp")
    return (gated_out / jnp.sqrt(totals[:, None] / C + 1e-05)).astype(jnp.bfloat16)


def solution(mesh):
    return jax.shard_map(
        local,
        mesh=mesh,
        in_specs=(P("seq", "mp"), P("seq", "mp"), P("seq", "mp"), P("seq", "mp"), P("mp")),
        out_specs=P("seq", "mp"),
        check_vma=False,
    )
```

profile of v0, /device:TPU:0, one launch (start us, length us, event | category | flops | bytes accessed | tf_op | source)
XLA Modules:
  0.0 116.8 jit_solution(7385291772707953139)
XLA Ops:
  0.0 1.9 %copy.17 = bf16[512,256]{0,1:T(8,128)(2,1)} copy(bf16[512,256]{1,0:T(8,128)(2,1)} %param.8) | data formatting | bytes 524288 | tf_op args[3]
  1.9 7.3 %all-to-all-start.1 = ((bf16[512,8,32]{0,2,1:T(8,128)(2,1)}), bf16[512,8,32]{0,2,1:T(8,128)(2,1)S(1)}, u32[]{:S(2)}, u32[]{:S(2)}) async-start(bf16[512,8,32]{0,2,1:T(8,128)(2,1)} %bitcast.5), calls=%async_computation.1 | async-start | bytes 524288 | tf_op jit(solution)/shard_map/all_to_all | solution.py:98
  9.2 1.2 %copy.12 = bf16[1024,256]{0,1:T(8,128)(2,1)S(1)} copy(bf16[1024,256]{1,0:T(8,128)(2,1)} %param.5) | data formatting | bytes 1048576 | tf_op args[0]
  10.5 0.0 copy-done
  10.5 0.2 copy.13
  10.7 0.5 negate_select_fusion.2
  11.2 0.3 select_multiply_fusion.1
  11.5 1.0 multiply_convert_fusion
  12.5 5.6 %all-to-all-done.1 = bf16[512,8,32]{0,2,1:T(8,128)(2,1)S(1)} async-done(((bf16[512,8,32]{0,2,1:T(8,128)(2,1)}), bf16[512,8,32]{0,2,1:T(8,128)(2,1)S(1)}, u32[]{:S(2)}, u32[]{:S(2)}) %all-to-all-start.1) | async-done | bytes 262176 | tf_op jit(solution)/shard_map/all_to_all | solution.py:98
  18.1 3.6 %all-to-all-start = ((bf16[1024,8,32]{0,2,1:T(8,128)(2,1)}), bf16[1024,8,32]{0,2,1:T(8,128)(2,1)S(1)}, u32[]{:S(2)}, u32[]{:S(2)}) async-start(bf16[1024,8,32]{0,2,1:T(8,128)(2,1)} %bitcast.1), calls=%async_computation | async-start | bytes 1048576 | tf_op jit(solution)/shard_map/all_to_all | solution.py:97
  21.7 0.1 copy.18
  21.8 0.2 reshape.98
  22.0 0.1 copy.19
  22.1 0.3 fusion.33
  22.4 0.3 fusion.39
  22.7 0.2 add_bitcast_fusion
  22.9 0.1 fusion.50
  23.0 0.1 maximum_bitcast_fusion
  23.1 0.1 maximum_bitcast_fusion.1
  23.2 0.1 pad_maximum_fusion
  23.3 1.5 %rev.3 = f32[32,32,256,2]{2,1,0,3:T(8,128)} reverse(f32[32,32,256,2]{2,1,0,3:T(8,128)S(1)} %pad_maximum_fusion), dimensions={0} | reverse | bytes 4194304 | tf_op jit(solution)/shard_map/rev | solution.py:69
  24.8 2.8 %reshape.99 = f32[32,1,8192,2]{2,0,3,1:T(8,128)} reshape(f32[32,32,256,2]{2,1,0,3:T(8,128)} %rev.3) | data formatting | bytes 4194304 | tf_op jit(solution)/shard_map/reshape
  27.6 8.2 %all-to-all-done = bf16[1024,8,32]{0,2,1:T(8,128)(2,1)S(1)} async-done(((bf16[1024,8,32]{0,2,1:T(8,128)(2,1)}), bf16[1024,8,32]{0,2,1:T(8,128)(2,1)S(1)}, u32[]{:S(2)}, u32[]{:S(2)}) %all-to-all-start) | async-done | bytes 524320 | tf_op jit(solution)/shard_map/all_to_all | solution.py:97
  35.9 0.2 fusion.14
  36.1 0.2 bitcast_dynamic-update-slice_fusion.1
  36.3 0.3 bitcast_dynamic-update-slice_fusion
  36.6 0.6 fusion.17
  37.2 0.6 convolution_add_fusion
  37.7 4.8 %reshape.109 = f32[1,95,8192,1]{2,0,3,1:T(1,128)} reshape(f32[95,32,256]{2,1,0:T(8,128)S(1)} %convolution_add_fusion) | data formatting | bytes 6225920 | tf_op jit(solution)/shard_map/reshape.1
  42.6 32.3 %convolution_reduce_fusion = f32[64,8192,2]{1,2,0:T(2,128)} fusion(f32[1,95,8192,1]{2,0,3,1:T(1,128)} %reshape.109, f32[32,1,8192,2]{2,0,3,1:T(8,128)} %reshape.99), kind=kOutput, calls=%fused_computation | convolution fusion | flops 201326592 | bytes 9404416 | tf_op jit(solution)/shard_map/convolution
  74.9 6.6 %reshape.100 = f32[64,32,256,2]{2,1,3,0:T(8,128)} reshape(f32[64,8192,2]{1,2,0:T(2,128)} %convolution_reduce_fusion) | data formatting | bytes 8388608 | tf_op jit(solution)/shard_map/reshape | solution.py:81
  81.6 2.5 %fusion.49 = (f32[64,32,256,1]{2,1,3,0:T(8,128)S(1)}, f32[64,32,256,1]{2,1,3,0:T(8,128)S(1)}) fusion(f32[64,32,256,2]{2,1,3,0:T(8,128)} %reshape.100), kind=kLoop, calls=%fused_computation.83 | loop fusion | bytes 8388608 | tf_op jit(solution)/shard_map/slice | solution.py:83
  84.1 1.2 %copy.38 = f32[64,32,256,1]{2,0,1,3:T(8,128)S(1)} copy(f32[64,32,256,1]{2,1,3,0:T(8,128)S(1)} %get-tuple-element.7) | data formatting | bytes 4194304
  85.3 1.2 %copy.39 = f32[64,32,256,1]{2,0,1,3:T(8,128)S(1)} copy(f32[64,32,256,1]{2,1,3,0:T(8,128)S(1)} %get-tuple-element.8) | data formatting | bytes 4194304
  86.6 0.3 slice_subtract_fusion
  86.9 1.0 fusion.8
  87.9 0.0 copy-start.1
  87.9 0.0 copy-start.2
  87.9 0.2 convert_element_type.80
  88.2 1.1 copy.25
  89.3 3.6 %all-to-all-start.2 = ((bf16[8,1024,32]{1,2,0:T(8,128)(2,1)}), bf16[8,1024,32]{1,2,0:T(8,128)(2,1)S(1)}, u32[]{:S(2)}, u32[]{:S(2)}) async-start(bf16[8,1024,32]{1,2,0:T(8,128)(2,1)} %copy.25), calls=%async_computation.2 | async-start | bytes 1048576 | tf_op jit(solution)/shard_map/all_to_all | solution.py:104
  92.9 0.0 copy-done.1
  92.9 0.2 copy.11
  93.1 14.2 %all-to-all-done.2 = bf16[8,1024,32]{1,2,0:T(8,128)(2,1)S(1)} async-done(((bf16[8,1024,32]{1,2,0:T(8,128)(2,1)}), bf16[8,1024,32]{1,2,0:T(8,128)(2,1)S(1)}, u32[]{:S(2)}, u32[]{:S(2)}) %all-to-all-start.2) | async-done | bytes 524320 | tf_op jit(solution)/shard_map/all_to_all | solution.py:104
  107.3 1.4 %multiply_reduce_fusion = f32[1024]{0:T(1024)S(1)} fusion(bf16[1024,256]{0,1:T(8,128)(2,1)} %multiply_convert_fusion, f32[256]{0:T(256)S(1)} %copy-done.2, bf16[1024,256]{0,1:T(8,128)(2,1)S(1)} %copy.11, bf16[8,1024,32]{1,2,0:T(8,128)(2,1)S(1)} %all-to-all-done.2), kind=kLoop, calls=%fused_computation.20 | loop fusion | flops 2096128 | bytes 1577984 | tf_op jit(solution)/shard_map/reduce_sum | solution.py:110
  108.7 5.7 %psum.7 = f32[1024]{0:T(1024)S(1)} all-reduce(f32[1024]{0:T(1024)S(1)} %multiply_reduce_fusion), channel_id=1, replica_groups=mesh['seq'=8,'mp'=4] {'mp'}, use_global_device_ids=true, to_apply=%region_1.2 | all-reduce | flops 1024 | bytes 8192 | tf_op jit(solution)/shard_map/psum | solution.py:111
  114.4 1.4 %divide_convert_fusion = bf16[1024,256]{0,1:T(8,128)(2,1)S(1)} fusion(f32[1024]{0:T(1024)S(1)} %add_sqrt_fusion, bf16[1024,256]{0,1:T(8,128)(2,1)} %multiply_convert_fusion, f32[256]{0:T(256)S(1)} %copy-done.2, bf16[1024,256]{0,1:T(8,128)(2,1)S(1)} %copy.11, bf16[8,1024,32]{1,2,0:T(8,128)(2,1)S(1)} %all-to-all-done.2), kind=kLoop, calls=%fused_computation.19 | loop fusion | flops 2097152 | bytes 2102272 | tf_op jit(solution)/shard_map/convert_element_type | solution.py:112
  115.8 1.0 copy.26
  (8 shorter events, 0.1 us)
Async XLA Ops:
  0.0 10.5 %copy-start = (bf16[1024,256]{1,0:T(8,128)(2,1)S(1)}, bf16[1024,256]{1,0:T(8,128)(2,1)}, u32[]{:S(2)}) copy-start(bf16[1024,256]{1,0:T(8,128)(2,1)} %param.6) | copy-start | bytes 1572868
  1.9 16.2 %all-to-all-start.1 = ((bf16[512,8,32]{0,2,1:T(8,128)(2,1)}), bf16[512,8,32]{0,2,1:T(8,128)(2,1)S(1)}, u32[]{:S(2)}, u32[]{:S(2)}) async-start(bf16[512,8,32]{0,2,1:T(8,128)(2,1)} %bitcast.5), calls=%async_computation.1 | async-start | bytes 524288 | tf_op jit(solution)/shard_map/all_to_all | solution.py:98
  18.1 17.8 %all-to-all-start = ((bf16[1024,8,32]{0,2,1:T(8,128)(2,1)}), bf16[1024,8,32]{0,2,1:T(8,128)(2,1)S(1)}, u32[]{:S(2)}, u32[]{:S(2)}) async-start(bf16[1024,8,32]{0,2,1:T(8,128)(2,1)} %bitcast.1), calls=%async_computation | async-start | bytes 1048576 | tf_op jit(solution)/shard_map/all_to_all | solution.py:97
  87.9 5.0 %copy-start.1 = (bf16[1024,256]{1,0:T(8,128)(2,1)S(1)}, bf16[1024,256]{1,0:T(8,128)(2,1)}, u32[]{:S(2)}) copy-start(bf16[1024,256]{1,0:T(8,128)(2,1)} %param.7) | copy-start | bytes 1572868
  87.9 19.4 %copy-start.2 = (f32[256]{0:T(256)S(1)}, f32[256]{0:T(256)}, u32[]{:S(2)}) copy-start(f32[256]{0:T(256)} %param.9) | copy-start | bytes 3076
  89.3 18.0 %all-to-all-start.2 = ((bf16[8,1024,32]{1,2,0:T(8,128)(2,1)}), bf16[8,1024,32]{1,2,0:T(8,128)(2,1)S(1)}, u32[]{:S(2)}, u32[]{:S(2)}) async-start(bf16[8,1024,32]{1,2,0:T(8,128)(2,1)} %copy.25), calls=%async_computation.2 | async-start | bytes 1048576 | tf_op jit(solution)/shard_map/all_to_all | solution.py:104
where the time goes:
time: 118 us; the launch traced here: 117 us
  matrix products  35.1 us (30%)
  waiting for transfers between devices  28 us (24%)
  local copies, waits for them, and re-layouts  27.9 us (24%)
  starting transfers between devices  14.5 us (12%)
  blocking collectives  5.67 us (5%)
  other arithmetic  5.42 us (5%)
    another operation x1, matrix products  32.3 us
    all_to_all x1, waiting for transfers between devices, local(): lax.all_to_all(shortened(channel_result), 'seq', split_axis=0, concat_axi...  14.2 us
    all_to_all x1, waiting for transfers between devices, local(): lax.all_to_all(gated, 'seq', split_axis=1, concat_axis=0, tiled=True)  8.22 us
    all_to_all x1, starting transfers between devices, local(): lax.all_to_all(filter_taps, 'seq', split_axis=1, concat_axis=0, tiled=True)  7.31 us
    reshape x1, local copies, waits for them, and re-layouts, convolve(): merged = merged.reshape(-1, channels, 2 * P_SIZE, 2)  6.65 us
    unnamed x14, local copies, waits for them, and re-layouts  6.38 us
    psum x1, blocking collectives, local(): totals = lax.psum(squares, 'mp')  5.67 us
    all_to_all x1, waiting for transfers between devices, local(): lax.all_to_all(filter_taps, 'seq', split_axis=1, concat_axis=0, tiled=True)  5.57 us
  transfers between devices with their start and end apart: 3, of which 3 were waited for; matrix products, arithmetic and copies ran while one was open for 8% of the time, Pallas kernels for 0%

commit v1 on v0

v1 whole, which is shorter than its diff:
```python
import functools

import jax
import jax.numpy as jnp
from jax import lax
from jax.experimental import pallas as pl
from jax.experimental.pallas import tpu as pltpu
from jax.sharding import PartitionSpec as P

MESH = pl.DeviceIdType.MESH
LANES = 128
TAPS, GATED, RESULT = 0, 1, 2
EPS = 1e-05


def peer_of(me, k, n):
    if n & (n - 1) == 0:
        return me ^ k
    return lax.rem(me + k, n)


def source_of(me, k, n):
    if n & (n - 1) == 0:
        return me ^ k
    return lax.rem(me + n - k, n)


def kernel(cfg, gate, value, og, taps, skip, out, stage, xm, hm, xr, hr, hf, xpad, rs, cr, ogt,
           mixed, power, powers, send_sem, recv_sem, own_sem, psend_sem, precv_sem):
    n, m, channels, blocks, cl, width, groups, sent_taps, hs, he, total_c = cfg
    me = lax.axis_index("seq")
    mine = lax.axis_index("mp")
    nd = hs * he
    order = list(range(n - 1, 0, -1))

    barrier = pltpu.get_barrier_semaphore()
    for k in range(1, n):
        pl.semaphore_signal(barrier, inc=1, device_id={"seq": peer_of(me, k, n)}, device_id_type=MESH)
    for k in range(1, m):
        pl.semaphore_signal(barrier, inc=1, device_id={"mp": peer_of(mine, k, m)}, device_id_type=MESH)

    if sent_taps:
        for e in range(he):
            part = taps[e * LANES:(e + 1) * LANES, :].astype(jnp.float32)
            stage[pl.ds(e, channels, stride=he), :] = part.T
        hm[...] = stage[: channels * he, :].astype(jnp.bfloat16).reshape(hm.shape)
    for a in range(blocks):
        span = slice(a * LANES, (a + 1) * LANES)
        part = gate[span, :].astype(jnp.float32) * value[span, :].astype(jnp.float32)
        stage[pl.ds(a, channels, stride=blocks), :] = part.T
    xm[...] = stage[...].astype(jnp.bfloat16).reshape(xm.shape)

    pl.semaphore_wait(barrier, n - 1 + m - 1)

    def rows_of(kind, g):
        per = he if kind == TAPS else blocks
        return pl.ds(g * width * per, width * per)

    def refs(kind):
        return {TAPS: (hm, hr), GATED: (xm, xr), RESULT: (rs, cr)}[kind]

    def remote(kind, g, k):
        src, dst = refs(kind)
        to = peer_of(me, k, n)
        rows = rows_of(kind, g)
        return pltpu.make_async_remote_copy(
            src_ref=src.at[to, rows],
            dst_ref=dst.at[me, rows],
            send_sem=send_sem.at[kind, g, k],
            recv_sem=recv_sem.at[kind, g, k],
            device_id={"seq": to},
            device_id_type=MESH,
        )

    def arrival(kind, g, k):
        src, dst = refs(kind)
        whence = source_of(me, k, n)
        rows = rows_of(kind, g)
        return pltpu.make_async_remote_copy(
            src_ref=src.at[whence, rows],
            dst_ref=dst.at[whence, rows],
            send_sem=send_sem.at[kind, g, k],
            recv_sem=recv_sem.at[kind, g, k],
            device_id={"seq": whence},
            device_id_type=MESH,
        )

    def own(kind, g):
        src, dst = refs(kind)
        rows = rows_of(kind, g)
        return pltpu.make_async_copy(src.at[me, rows], dst.at[me, rows], own_sem.at[kind, g])

    forward = ([TAPS] if sent_taps else []) + [GATED]
    for g in range(groups):
        for kind in forward:
            for k in order:
                remote(kind, g, k).start()
            own(kind, g).start()

    for a in range(blocks):
        span = slice(a * LANES, (a + 1) * LANES)
        ogt[pl.ds(a, channels, stride=blocks), :] = og[span, :].astype(jnp.float32).T
    xpad[:, :nd, :] = jnp.zeros((2, nd, LANES), jnp.float32)

    lane = lax.broadcasted_iota(jnp.int32, (16, LANES), 1)
    sub = lax.broadcasted_iota(jnp.int32, (16, LANES), 0)
    total = n * blocks

    def toeplitz(c):
        lines = []
        for d in range(nd):
            source = hf if sent_taps else taps
            line = source[d // he, pl.ds(c * he + d % he, 1), :]
            line = jnp.broadcast_to(line, (16, LANES))
            lines.append(pltpu.roll(line, 0, 1, stride=1, stride_axis=0))
        zero = jnp.zeros((16, LANES), jnp.float32)
        first = []
        for d in range(nd + 1):
            here = lines[d] if d < nd else zero
            before = lines[d - 1] if d > 0 else zero
            first.append(jnp.where(lane >= sub, here, before))
        tiles = []
        turned = [[(f if q == 0 else pltpu.roll(f, 16 * q, 1)) for q in range(8)] for f in first]
        for d in range(nd + 1):
            rows = []
            for q in range(8):
                before = turned[d - 1][q] if d > 0 else zero
                rows.append(turned[d][q] if q == 0 else jnp.where(lane >= 16 * q, turned[d][q], before))
            tiles.append(jnp.concatenate(rows, axis=0).astype(jnp.bfloat16))
        return tiles

    def one_pair(base, p):
        c0 = base + 2 * p
        start = pl.multiple_of(c0 * blocks, 2 * blocks)
        both = xr[:, pl.ds(start, 2 * blocks), :].astype(jnp.float32)
        results = []
        for e in range(2):
            rows = both[:, e * blocks:(e + 1) * blocks, :].reshape(total, LANES)
            xpad[e, nd:, :] = rows
            tiles = toeplitz(c0 + e)
            acc = rows * skip[me * cl + c0 + e]
            for d in range(0, nd + 1, 2):
                ds = [d, d + 1] if d + 1 <= nd else [d]
                left = [xpad[e, nd - x:nd - x + total, :].astype(jnp.bfloat16) for x in ds]
                left = left[0] if len(ds) == 1 else jnp.concatenate(left, axis=1)
                right = tiles[d] if len(ds) == 1 else jnp.concatenate([tiles[d], tiles[d + 1]], axis=0)
                acc = acc + jnp.dot(left, right, preferred_element_type=jnp.float32)
            results.append(acc.reshape(n, blocks, LANES))
        rs[:, pl.ds(start, 2 * blocks), :] = jnp.concatenate(results, axis=1).astype(jnp.bfloat16)

    for g in range(groups):
        for kind in forward:
            own(kind, g).wait()
            for k in order:
                arrival(kind, g, k).wait_recv()
        if sent_taps:
            rows = rows_of(TAPS, g)
            hf[:, rows, :] = hr[:, rows, :].astype(jnp.float32)

        def step(p, carry):
            one_pair(g * width, p)
            return carry

        lax.fori_loop(0, width // 2, step, 0)
        for k in order:
            remote(RESULT, g, k).start()
        own(RESULT, g).start()

    power[...] = jnp.zeros_like(power)
    for g in range(groups):
        own(RESULT, g).wait()
        for k in order:
            arrival(RESULT, g, k).wait_recv()

        def gather(d, carry):
            rows = rows_of(RESULT, g)
            at = pl.multiple_of(d * cl * blocks + g * width * blocks, width * blocks)
            piece = ogt[pl.ds(at, width * blocks), :] * cr[d, rows, :].astype(jnp.float32)
            mixed[pl.ds(at, width * blocks), :] = piece
            square = (piece * piece).reshape(width, blocks, LANES)
            power[...] += jnp.sum(square, axis=0)
            return carry

        lax.fori_loop(0, n, gather, 0)

    def exchange(k, incoming):
        other = source_of(mine, k, m) if incoming else peer_of(mine, k, m)
        return pltpu.make_async_remote_copy(
            src_ref=power,
            dst_ref=powers.at[other if incoming else mine],
            send_sem=psend_sem.at[k],
            recv_sem=precv_sem.at[k],
            device_id={"mp": other},
            device_id_type=MESH,
        )

    for k in range(1, m):
        exchange(k, False).start()
    for kind in forward + [RESULT]:
        for g in range(groups):
            for k in order:
                remote(kind, g, k).wait_send()
    for k in range(1, m):
        exchange(k, True).wait_recv()
    sums = power[...]
    for k in range(1, m):
        sums = sums + powers[source_of(mine, k, m)]
    scale = 1.0 / jnp.sqrt(sums / total_c + EPS)
    for a in range(blocks):
        part = mixed[pl.ds(a, channels, stride=blocks), :] * scale[a:a + 1, :]
        out[a * LANES:(a + 1) * LANES, :] = part.T.astype(jnp.bfloat16)
    for k in range(1, m):
        exchange(k, False).wait_send()


def solution(mesh):
    n, m = mesh.shape["seq"], mesh.shape["mp"]

    def local(gate_in, value_in, out_gate, filter_taps, skip_gain):
        tokens, channels = gate_in.shape
        blocks = tokens // LANES
        cl = channels // n
        width = min(cl, 8)
        groups = cl // width
        own_taps = filter_taps.shape[0]
        sent_taps = own_taps % LANES == 0 and (width * (own_taps // LANES)) % 16 == 0
        nd = own_taps * n // LANES
        if sent_taps:
            hs, he, taps = n, own_taps // LANES, filter_taps
        else:
            hs, he = 1, nd
            moved = lax.all_to_all(filter_taps, "seq", split_axis=1, concat_axis=0, tiled=True)
            taps = moved.astype(jnp.float32).T.reshape(1, cl * nd, LANES)
        cfg = (n, m, channels, blocks, cl, width, groups, sent_taps, hs, he, channels * m)
        vmem = pl.BlockSpec(memory_space=pltpu.VMEM)
        message = (n, cl * blocks, LANES)
        taps_message = (n, cl * he, LANES) if sent_taps else (n, 16, LANES)
        return pl.pallas_call(
            functools.partial(kernel, cfg),
            out_shape=jax.ShapeDtypeStruct((tokens, channels), jnp.bfloat16),
            in_specs=[vmem, vmem, vmem, vmem, pl.BlockSpec(memory_space=pltpu.SMEM)],
            out_specs=vmem,
            scratch_shapes=[
                pltpu.VMEM((channels * blocks, LANES), jnp.float32),
                pltpu.VMEM(message, jnp.bfloat16),
                pltpu.VMEM(taps_message, jnp.bfloat16),
                pltpu.VMEM(message, jnp.bfloat16),
                pltpu.VMEM(taps_message, jnp.bfloat16),
                pltpu.VMEM(taps_message, jnp.float32),
                pltpu.VMEM((2, nd + n * blocks, LANES), jnp.float32),
                pltpu.VMEM(message, jnp.bfloat16),
                pltpu.VMEM(message, jnp.bfloat16),
                pltpu.VMEM((channels * blocks, LANES), jnp.float32),
                pltpu.VMEM((channels * blocks, LANES), jnp.float32),
                pltpu.VMEM((blocks, LANES), jnp.float32),
                pltpu.VMEM((m, blocks, LANES), jnp.float32),
                pltpu.SemaphoreType.DMA((3, groups, n)),
                pltpu.SemaphoreType.DMA((3, groups, n)),
                pltpu.SemaphoreType.DMA((3, groups)),
                pltpu.SemaphoreType.DMA((m,)),
                pltpu.SemaphoreType.DMA((m,)),
            ],
            compiler_params=pltpu.CompilerParams(
                collective_id=0, has_side_effects=True, vmem_limit_bytes=48 * 1024 * 1024
            ),
        )(gate_in, value_in, out_gate, taps, skip_gain)

    return jax.shard_map(
        local,
        mesh=mesh,
        in_specs=(P("seq", "mp"), P("seq", "mp"), P("seq", "mp"), P("seq", "mp"), P("mp")),
        out_specs=P("seq", "mp"),
        check_vma=False,
    )
```

time: 118 us -> 48.3 us (0.41)
  Pallas kernels: 0 us -> 42.4 us
  matrix products: 35.1 us -> 0 us
  waiting for transfers between devices: 28 us -> 0 us
  local copies, waits for them, and re-layouts: 27.9 us -> 5.55 us
  starting transfers between devices: 14.5 us -> 0 us
  blocking collectives: 5.67 us -> 0 us
  other arithmetic: 5.42 us -> 0 us
    pallas_call x0 -> x1, Pallas kernels: none -> 42.4 us  [local(): pl.pallas_call(functools.partial(kernel, cfg), out_shape=jax.ShapeDtypeSt...]
    another operation x1 -> x0, matrix products: 32.3 us -> none
    all_to_all x3 -> x0, waiting for transfers between devices: 28 us -> none  [the longest x1 14.2 us: local(): lax.all_to_all(shortened(channel_result), 'seq', split_axis=0, concat_axi...]
    all_to_all x3 -> x0, starting transfers between devices: 14.5 us -> none  [the longest x1 7.31 us: local(): lax.all_to_all(filter_taps, 'seq', split_axis=1, concat_axis=0, tiled=True)]
    reshape x4 -> x0, local copies, waits for them, and re-layouts: 9.71 us -> none  [the longest x1 6.65 us: convolve(): merged = merged.reshape(-1, channels, 2 * P_SIZE, 2)]
    psum x1 -> x0, blocking collectives: 5.67 us -> none  [local(): totals = lax.psum(squares, 'mp')]
    another operation x1 -> x0, local copies, waits for them, and re-layouts: 4.83 us -> none
    slice x2 -> x0, local copies, waits for them, and re-layouts: 2.68 us -> none  [the longest x1 2.55 us: convolve(): with_imag = merged[..., 1]]
  transfers between devices with their start and end apart: 3 -> 0, of which waited for: 3 -> 0; matrix products, arithmetic and copies ran while one was open for 8% -> 0% of each run, Pallas kernels for 0% -> 0%
where the time goes in v1:
time: 48.3 us; the launch traced here: 48 us
  Pallas kernels  42.4 us (88%)
  local copies, waits for them, and re-layouts  5.55 us (11%)
    pallas_call x1, Pallas kernels, local(): pl.pallas_call(functools.partial(kernel, cfg), out_shape=jax.ShapeDtypeSt...  42.4 us
    unnamed x11, local copies, waits for them, and re-layouts  5.55 us

profile of v1, /device:TPU:0, one launch (start us, length us, event | category | flops | bytes accessed | tf_op | source)
XLA Modules:
  0.0 48.0 jit_solution(8807544084068337365)
XLA Ops:
  0.0 0.0 copy-start
  0.0 1.0 %copy-done = bf16[1024,256]{1,0:T(8,128)(2,1)S(1)} copy-done((bf16[1024,256]{1,0:T(8,128)(2,1)S(1)}, bf16[1024,256]{1,0:T(8,128)(2,1)}, u32[]{:S(2)}) %copy-start) | copy-done | bytes 524312
  1.0 0.0 copy-start.1
  1.0 1.0 %copy-done.1 = bf16[1024,256]{1,0:T(8,128)(2,1)S(1)} copy-done((bf16[1024,256]{1,0:T(8,128)(2,1)S(1)}, bf16[1024,256]{1,0:T(8,128)(2,1)}, u32[]{:S(2)}) %copy-start.1) | copy-done | bytes 524312
  2.1 0.0 copy-start.2
  2.1 1.0 %copy-done.2 = bf16[1024,256]{1,0:T(8,128)(2,1)S(1)} copy-done((bf16[1024,256]{1,0:T(8,128)(2,1)S(1)}, bf16[1024,256]{1,0:T(8,128)(2,1)}, u32[]{:S(2)}) %copy-start.2) | copy-done | bytes 524312
  3.1 0.0 copy-start.3
  3.1 0.9 %copy-done.3 = bf16[512,256]{1,0:T(8,128)(2,1)S(1)} copy-done((bf16[512,256]{1,0:T(8,128)(2,1)S(1)}, bf16[512,256]{1,0:T(8,128)(2,1)}, u32[]{:S(2)}) %copy-start.3) | copy-done | bytes 262168
  4.1 0.0 copy-start.4
  4.1 0.7 %copy-done.4 = f32[256]{0:T(256)S(1)} copy-done((f32[256]{0:T(256)S(1)}, f32[256]{0:T(256)}, u32[]{:S(2)}) %copy-start.4) | copy-done | bytes 1048
  4.8 42.4 %shard_map.55 = bf16[1024,256]{1,0:T(8,128)(2,1)S(1)} custom-call(bf16[1024,256]{1,0:T(8,128)(2,1)S(1)} %copy-done, bf16[1024,256]{1,0:T(8,128)(2,1)S(1)} %copy-done.1, bf16[1024,256]{1,0:T(8,128)(2,1)S(1)} %copy-done.2, bf16[512,256]{1,0:T(8,128)(2,1)S(1)} %copy-done.3, f32[256]{0:T(256)S(1)} %copy-done.4), custom_call_target="tpu_custom_call" | custom-call | tf_op jit(solution)/shard_map/pallas_call | solution.py:238
  47.2 0.8 %copy.7 = bf16[1024,256]{1,0:T(8,128)(2,1)} copy(bf16[1024,256]{1,0:T(8,128)(2,1)S(1)} %shard_map.55) | data formatting | bytes 1048576
Async XLA Ops:
  0.0 1.0 %copy-start = (bf16[1024,256]{1,0:T(8,128)(2,1)S(1)}, bf16[1024,256]{1,0:T(8,128)(2,1)}, u32[]{:S(2)}) copy-start(bf16[1024,256]{1,0:T(8,128)(2,1)} %gate.1) | copy-start | bytes 1572868
  1.0 1.0 %copy-start.1 = (bf16[1024,256]{1,0:T(8,128)(2,1)S(1)}, bf16[1024,256]{1,0:T(8,128)(2,1)}, u32[]{:S(2)}) copy-start(bf16[1024,256]{1,0:T(8,128)(2,1)} %value.1) | copy-start | bytes 1572868
  2.1 1.0 %copy-start.2 = (bf16[1024,256]{1,0:T(8,128)(2,1)S(1)}, bf16[1024,256]{1,0:T(8,128)(2,1)}, u32[]{:S(2)}) copy-start(bf16[1024,256]{1,0:T(8,128)(2,1)} %og.1) | copy-start | bytes 1572868
  3.1 0.9 %copy-start.3 = (bf16[512,256]{1,0:T(8,128)(2,1)S(1)}, bf16[512,256]{1,0:T(8,128)(2,1)}, u32[]{:S(2)}) copy-start(bf16[512,256]{1,0:T(8,128)(2,1)} %taps.1) | copy-start | bytes 786436
  4.1 0.7 %copy-start.4 = (f32[256]{0:T(256)S(1)}, f32[256]{0:T(256)}, u32[]{:S(2)}) copy-start(f32[256]{0:T(256)} %skip.1) | copy-start | bytes 3076

commit v2 on v1

--- a/solution.py
+++ b/solution.py
@@ -25,25 +25,38 @@
     return lax.rem(me + n - k, n)
 
 
-def kernel(cfg, gate, value, og, taps, skip, out, stage, xm, hm, xr, hr, hf, xpad, rs, cr, ogt,
-           mixed, power, powers, send_sem, recv_sem, own_sem, psend_sem, precv_sem):
+def kernel(cfg, gate_in, value_in, og_in, taps_in, skip_in, out, gate, value, og, taps, skip, stage,
+           xm, hm, xr, hr, hf, xpad, rs, cr, ogt, mixed, power, powers, load_sem, send_sem, recv_sem,
+           own_sem, psend_sem, precv_sem):
     n, m, channels, blocks, cl, width, groups, sent_taps, hs, he, total_c = cfg
     me = lax.axis_index("seq")
     mine = lax.axis_index("mp")
     nd = hs * he
     order = list(range(n - 1, 0, -1))
 
+    loads = [
+        pltpu.make_async_copy(src, dst, load_sem.at[i])
+        for i, (src, dst) in enumerate(
+            [(taps_in, taps), (gate_in, gate), (value_in, value), (og_in, og), (skip_in, skip)]
+        )
+    ]
+    for load in loads:
+        load.start()
+
     barrier = pltpu.get_barrier_semaphore()
     for k in range(1, n):
         pl.semaphore_signal(barrier, inc=1, device_id={"seq": peer_of(me, k, n)}, device_id_type=MESH)
     for k in range(1, m):
         pl.semaphore_signal(barrier, inc=1, device_id={"mp": peer_of(mine, k, m)}, device_id_type=MESH)
 
+    loads[0].wait()
     if sent_taps:
         for e in range(he):
             part = taps[e * LANES:(e + 1) * LANES, :].astype(jnp.float32)
             stage[pl.ds(e, channels, stride=he), :] = part.T
         hm[...] = stage[: channels * he, :].astype(jnp.bfloat16).reshape(hm.shape)
+    loads[1].wait()
+    loads[2].wait()
     for a in range(blocks):
         span = slice(a * LANES, (a + 1) * LANES)
         part = gate[span, :].astype(jnp.float32) * value[span, :].astype(jnp.float32)
@@ -97,6 +110,8 @@
                 remote(kind, g, k).start()
             own(kind, g).start()
 
+    loads[3].wait()
+    loads[4].wait()
     for a in range(blocks):
         span = slice(a * LANES, (a + 1) * LANES)
         ogt[pl.ds(a, channels, stride=blocks), :] = og[span, :].astype(jnp.float32).T
@@ -118,15 +133,16 @@
         for d in range(nd + 1):
             here = lines[d] if d < nd else zero
             before = lines[d - 1] if d > 0 else zero
-            first.append(jnp.where(lane >= sub, here, before))
+            first.append(jnp.where(lane >= sub, here, before).astype(jnp.bfloat16))
+        none = jnp.zeros((16, LANES), jnp.bfloat16)
         tiles = []
         turned = [[(f if q == 0 else pltpu.roll(f, 16 * q, 1)) for q in range(8)] for f in first]
         for d in range(nd + 1):
             rows = []
             for q in range(8):
-                before = turned[d - 1][q] if d > 0 else zero
+                before = turned[d - 1][q] if d > 0 else none
                 rows.append(turned[d][q] if q == 0 else jnp.where(lane >= 16 * q, turned[d][q], before))
-            tiles.append(jnp.concatenate(rows, axis=0).astype(jnp.bfloat16))
+            tiles.append(jnp.concatenate(rows, axis=0))
         return tiles
 
     def one_pair(base, p):
@@ -238,9 +254,14 @@
         return pl.pallas_call(
             functools.partial(kernel, cfg),
             out_shape=jax.ShapeDtypeStruct((tokens, channels), jnp.bfloat16),
-            in_specs=[vmem, vmem, vmem, vmem, pl.BlockSpec(memory_space=pltpu.SMEM)],
+            in_specs=[pl.BlockSpec(memory_space=pltpu.HBM)] * 5,
             out_specs=vmem,
             scratch_shapes=[
+                pltpu.VMEM(gate_in.shape, gate_in.dtype),
+                pltpu.VMEM(value_in.shape, value_in.dtype),
+                pltpu.VMEM(out_gate.shape, out_gate.dtype),
+                pltpu.VMEM(taps.shape, taps.dtype),
+                pltpu.SMEM(skip_gain.shape, skip_gain.dtype),
                 pltpu.VMEM((channels * blocks, LANES), jnp.float32),
                 pltpu.VMEM(message, jnp.bfloat16),
                 pltpu.VMEM(taps_message, jnp.bfloat16),
@@ -254,6 +275,7 @@
                 pltpu.VMEM((channels * blocks, LANES), jnp.float32),
                 pltpu.VMEM((blocks, LANES), jnp.float32),
                 pltpu.VMEM((m, blocks, LANES), jnp.float32),
+                pltpu.SemaphoreType.DMA((5,)),
                 pltpu.SemaphoreType.DMA((3, groups, n)),
                 pltpu.SemaphoreType.DMA((3, groups, n)),
                 pltpu.SemaphoreType.DMA((3, groups)),
@@ -261,7 +283,7 @@
                 pltpu.SemaphoreType.DMA((m,)),
             ],
             compiler_params=pltpu.CompilerParams(
-                collective_id=0, has_side_effects=True, vmem_limit_bytes=48 * 1024 * 1024
+                collective_id=0, has_side_effects=True, vmem_limit_bytes=67043328
             ),
         )(gate_in, value_in, out_gate, taps, skip_gain)
 

time: 48.3 us -> 44.7 us (0.925)
  local copies, waits for them, and re-layouts: 5.55 us -> 1.87 us
    unnamed x11 -> x1, local copies, waits for them, and re-layouts: 5.55 us -> 1.87 us
where the time goes in v2:
time: 44.7 us; the launch traced here: 44.5 us
  Pallas kernels  42.6 us (95%)
  local copies, waits for them, and re-layouts  1.87 us (4%)
    pallas_call x1, Pallas kernels, local(): pl.pallas_call(functools.partial(kernel, cfg), out_shape=jax.ShapeDtypeSt...  42.6 us
    unnamed x1, local copies, waits for them, and re-layouts  1.87 us

profile of v2, /device:TPU:0, one launch (start us, length us, event | category | flops | bytes accessed | tf_op | source)
XLA Modules:
  0.0 44.5 jit_solution(6274316428725376376)
XLA Ops:
  0.0 42.6 %shard_map.55 = bf16[1024,256]{1,0:T(8,128)(2,1)} custom-call(bf16[1024,256]{1,0:T(8,128)(2,1)} %gate_in.1, bf16[1024,256]{1,0:T(8,128)(2,1)} %value_in.1, bf16[1024,256]{1,0:T(8,128)(2,1)} %og_in.1, bf16[512,256]{1,0:T(8,128)(2,1)} %taps_in.1, f32[256]{0:T(256)} %skip_in.1), custom_call_target="tpu_custom_call" | custom-call | tf_op jit(solution)/shard_map/pallas_call | solution.py:254
  42.6 1.9 %copy.7 = bf16[1024,256]{1,0:T(8,128)(2,1)} copy(bf16[1024,256]{1,0:T(8,128)(2,1)} %shard_map.55) | data formatting | bytes 1048576
